TPU v7x, 512 devices: a whole 4x4x16 slice. The times are simulated.
512 devices in a mesh: leaf: 32 (over z_hi, x, core), group: 16 (over y, z_lo).
Axes of the slice: x: 4, y: 4, z: 16 (z_hi: 4, z_lo: 4; z = z_hi * 4 + z_lo), core: 2. Of those that a mesh axis runs over, the one named last changes fastest.
Arguments:
- coefficients: float32 [16, 4096, 512], P('group', 'leaf'), may hold values from -6 to 6
- labels: float32 [16, 4096, 512], P('group', 'leaf'), may hold values from -6 to 6
- near_kernel: float32 [16, 4096, 3072], P('group', 'leaf'), may hold values from -0.109375 to 0.109375
- basis: float32 [16, 4096, 256], P('group', 'leaf'), may hold values from -0.1875 to 0.1875
- transfer: float32 [16, 1024, 256], P('group', 'leaf'), may hold values from -0.375 to 0.375
- coupling: float32 [16, 256, 4096], P('group', 'leaf'), may hold values from -0.09375 to 0.09375
- near_lists: int32 [16, 4, 3], P('group'), may hold values from 0 to 3, as said below
- ridge: float32 [1], replicated, may hold values from 0.5 to 2
Outputs:
- residual: float32 [16, 4096, 512], P('group', 'leaf')
Inputs may be any that keep to these rules, and one draw needn't show every extreme that they name: `near_lists`: entry 0 of each leaf's list is the leaf itself; in each group the leaves lie on one cycle through all 4 leaves, and entries 1 and 2 of a leaf's list are its two neighbours on that cycle.
All inputs are finite; a program needn't handle non-finite values.
Results may differ from a plain program's by a relative error of at most 0.0011.
Values may be sent and summed in bfloat16 or wider, within the bound.
A program may use at most 64 MiB of HBM per device.

v0:
```python
import jax
import jax.numpy as jnp
from jax import lax
from jax.sharding import Mesh
from jax.sharding import PartitionSpec as P

LPG = 4
LEAF = ("leaf_0", "leaf_1", "leaf_2")


def swapped(shard, axis, distance):
    return lax.ppermute(shard, axis, [(i, i ^ 1 << distance) for i in range(lax.axis_size(axis))])


def rows_for(lines, count):
    spare = -len(lines) % count
    return jnp.pad(lines, [(0, spare)] + [(0, 0)] * (lines.ndim - 1))


def from_everyone(shard, axis):
    copies = jnp.broadcast_to(shard, (lax.axis_size(axis), *shard.shape))
    return lax.all_to_all(copies, axis, split_axis=0, concat_axis=0, tiled=True)


def in_order(blocks, dim):
    blocks = jnp.moveaxis(blocks, 0, dim)
    dims = blocks.shape
    return blocks.reshape(*dims[:dim], dims[dim] * dims[dim + 1], *dims[dim + 2 :])


def whole_of(shard, axes, dim):
    far, near = axes
    blocks = from_everyone(from_everyone(shard, far), near)
    return in_order(blocks.swapaxes(0, 1).reshape(-1, *shard.shape), dim)


def in_blocks(shard, dim, count):
    dims = shard.shape
    blocks = shard.reshape(*dims[:dim], count, dims[dim] // count, *dims[dim + 1 :])
    return jnp.moveaxis(blocks, dim, 0)


def sum_at_owner(shard, axis, dim):
    count = lax.axis_size(axis)
    blocks = lax.all_to_all(in_blocks(shard, dim, count), axis, 0, 0, tiled=True)
    return jnp.sum(blocks, axis=0)


def sum_by_axis(shard, axes, dim):
    far, near = axes
    own = sum_at_owner(in_blocks(shard, dim, lax.axis_size(far)), near, dim + 1)
    return jnp.sum(lax.all_to_all(own, far, 0, 0, tiled=True), axis=0)


def total_of(shard, axes):
    lines = shard.reshape(-1, shard.shape[-1])
    padded = rows_for(lines, lax.axis_size(axes[0]) * lax.axis_size(axes[1]))
    whole = whole_of(sum_by_axis(padded, axes, 0), axes, 0)
    return lax.slice_in_dim(whole, 0, len(lines)).reshape(shard.shape)


def matmul(left, right):
    return jnp.dot(left, right, precision=lax.Precision.HIGHEST, preferred_element_type=jnp.float32)


def shards(coefficients, labels, near_kernel, basis, transfer, coupling, near_lists, ridge):
    local_coef = coefficients[0]
    column_count = local_coef.shape[1]
    leaf_split = lax.axis_size(LEAF) // LPG
    levels = leaf_split.bit_length() - 1
    position = lax.axis_index(LEAF)
    leaf_index = position // leaf_split
    chosen = lax.dynamic_index_in_dim(near_lists[0], leaf_index, 0, keepdims=False)
    local_kernel = near_kernel[0]
    list_length = chosen.shape[0]
    leaf_width = local_kernel.shape[1] // list_length
    group_all = lax.all_gather(coefficients, LEAF, axis=1, tiled=True)[0]
    leaf_blocks = group_all.reshape(group_all.shape[0] // leaf_width, leaf_width, column_count)
    selected = jnp.take(leaf_blocks, chosen, axis=0)
    near = matmul(local_kernel, selected.reshape(list_length * leaf_width, column_count))
    basis_rows = basis[0]
    partial_coef = matmul(basis_rows.T, local_coef)
    for bit_level in reversed(range(levels)):
        halfway = partial_coef.shape[0] // 2
        lower_half = partial_coef[:halfway]
        upper_half = partial_coef[halfway:]
        upper_side = position // (1 << bit_level) % 2 == 1
        kept = jnp.where(upper_side, upper_half, lower_half)
        given = jnp.where(upper_side, lower_half, upper_half)
        partial_coef = kept + swapped(given, LEAF, bit_level)
    contribution = matmul(transfer[0].T, partial_coef)
    coupling_rows = coupling[0]
    group_coef = total_of(contribution, (("leaf_0", "leaf_1"), "leaf_2"))
    group_round = group_coef.astype(jnp.bfloat16)
    coarse_part = matmul(
        coupling_rows, lax.all_gather(group_round, "group", axis=0, tiled=True).astype(jnp.float32)
    )
    coarse = lax.all_gather(coarse_part, LEAF, axis=0, tiled=True)
    slice_coarse = matmul(transfer[0], coarse)
    for bit_level in range(levels):
        partner = swapped(slice_coarse, LEAF, bit_level)
        upper_side = position // (1 << bit_level) % 2 == 1
        slice_coarse = jnp.where(
            upper_side,
            jnp.concatenate([partner, slice_coarse], axis=0),
            jnp.concatenate([slice_coarse, partner], axis=0),
        )
    far = matmul(basis_rows, slice_coarse)
    result = labels[0] - (near + far + ridge[0] * local_coef)
    return result[None]


def solution(mesh):
    finer = Mesh(
        mesh.devices.reshape(4, 4, 2, mesh.shape["group"]), ("leaf_0", "leaf_1", "leaf_2", "group")
    )
    placed = (
        P("group", LEAF, None),
        P("group", LEAF, None),
        P("group", LEAF, None),
        P("group", LEAF, None),
        P("group", LEAF, None),
        P("group", LEAF, None),
        P("group", None, None),
        P(),
    )
    return jax.shard_map(
        shards, mesh=finer, in_specs=placed, out_specs=P("group", LEAF, None), check_vma=False
    )
```

profile of v0, /device:TPU:1, one launch (start us, length us, event | category | flops | bytes accessed | tf_op | source)
XLA Modules:
  0.0 370.4 jit_solution(68292817109640035)
XLA Ops:
  6.6 1.8 fusion.11
  8.4 5.5 %collective-permute-start = (f32[128,512]{1,0:T(8,128)S(1)}, f32[128,512]{1,0:T(8,128)S(1)}, u32[]{:S(2)}, u32[]{:S(2)}) collective-permute-start(f32[128,512]{1,0:T(8,128)S(1)} %slice_select_fusion), channel_id=1, source_target_pairs={{0,64},{16,80},{32,96},{48,112},{64,0},{80,16},{96,32},{112,48},{1... | collective-permute-start | bytes 786440 | tf_op jit(solution)/shard_map/ppermute | solution.py:12
  13.9 3.7 %collective-permute-done = f32[128,512]{1,0:T(8,128)S(1)} collective-permute-done((f32[128,512]{1,0:T(8,128)S(1)}, f32[128,512]{1,0:T(8,128)S(1)}, u32[]{:S(2)}, u32[]{:S(2)}) %collective-permute-start) | collective-permute-done | bytes 262176 | tf_op jit(solution)/shard_map/ppermute | solution.py:12
  17.7 5.3 %collective-permute-start.1 = (f32[64,512]{1,0:T(8,128)S(1)}, f32[64,512]{1,0:T(8,128)S(1)}, u32[]{:S(2)}, u32[]{:S(2)}) collective-permute-start(f32[64,512]{1,0:T(8,128)S(1)} %slice_select_fusion.1), channel_id=1, source_target_pairs={{0,32},{16,48},{32,0},{48,16},{64,96},{80,112},{96,64},{112,80},{1... | collective-permute-start | bytes 393224 | tf_op jit(solution)/shard_map/ppermute | solution.py:12
  23.0 2.3 collective-permute-done.1
  25.4 8.6 %collective-permute-start.2 = (f32[32,512]{1,0:T(8,128)S(1)}, f32[32,512]{1,0:T(8,128)S(1)}, u32[]{:S(2)}, u32[]{:S(2)}) collective-permute-start(f32[32,512]{1,0:T(8,128)S(1)} %slice_select_fusion.2), channel_id=1, source_target_pairs={{0,16},{16,0},{32,48},{48,32},{64,80},{80,64},{96,112},{112,96},{1... | collective-permute-start | bytes 196616 | tf_op jit(solution)/shard_map/ppermute | solution.py:12
  34.9 1.4 fusion.17
  36.4 4.3 %all_to_all.20 = f32[2,16,8,512]{3,2,1,0:T(8,128)S(1)} all-to-all(f32[2,16,8,512]{3,2,1,0:T(8,128)S(1)} %bitcast.62), channel_id=1, replica_groups=mesh['leaf_0'=4,'leaf_1'=4,'leaf_2'=2,'group'=16] {'leaf_2'}, dimensions={0} | all-to-all | bytes 1048576 | tf_op jit(solution)/shard_map/all_to_all | solution.py:45
  40.7 29.3 %all_to_all.21 = f32[16,8,512]{2,1,0:T(8,128)S(1)} all-to-all(f32[16,8,512]{2,1,0:T(8,128)S(1)} %reduce_sum.18), channel_id=1, replica_groups=mesh['leaf_0'=4,'leaf_1'=4,'leaf_2'=2,'group'=16] {'leaf_0','leaf_1'}, dimensions={0} | all-to-all | bytes 524288 | tf_op jit(solution)/shard_map/all_to_all | solution.py:52
  70.0 24.6 %all_to_all.22 = bf16[16,8,512]{2,1,0:T(8,128)(2,1)S(1)} all-to-all(bf16[16,8,512]{2,1,0:T(8,128)(2,1)S(1)} %broadcast_in_dim.21), channel_id=1, replica_groups=mesh['leaf_0'=4,'leaf_1'=4,'leaf_2'=2,'group'=16] {'leaf_0','leaf_1'}, dimensions={0} | all-to-all | bytes 262144 | tf_op jit(solution)/shard_map/all_to_all | solution.py:22
  94.7 6.4 %all_to_all.23 = bf16[2,16,8,512]{3,2,1,0:T(8,128)(2,1)S(1)} all-to-all(bf16[2,16,8,512]{3,2,1,0:T(8,128)(2,1)S(1)} %broadcast_in_dim.22), channel_id=1, replica_groups=mesh['leaf_0'=4,'leaf_1'=4,'leaf_2'=2,'group'=16] {'leaf_2'}, dimensions={0} | all-to-all | bytes 524288 | tf_op jit(solution)/shard_map/all_to_all | solution.py:22
  102.9 97.5 %all-gather.5.cloned.1.call-done = bf16[4096,512]{1,0:T(8,128)(2,1)} async-done(((bf16[256,512]{1,0:T(8,128)(2,1)}), bf16[4096,512]{1,0:T(8,128)(2,1)}) %all-gather.5.cloned.1.call-update) | async-done | bytes 4194320 | tf_op jit(solution)/shard_map/all_gather | solution.py:96
  200.4 3.9 %convolution_bitcast_fusion.1 = f32[8,512]{1,0:T(8,128)S(1)} fusion(bf16[4096,512]{1,0:T(8,128)(2,1)} %all-gather.5.cloned.1.call-done, f32[1,8,4096]{2,1,0:T(8,128)S(1)} %copy-done.4), kind=kOutput, calls=%fused_computation.10 | convolution fusion | flops 201326592 | bytes 4341760 | tf_op jit(solution)/shard_map/dot_general | solution.py:63
  204.3 58.1 %all_gather.11 = f32[256,512]{1,0:T(8,128)S(1)} all-gather(f32[8,512]{1,0:T(8,128)S(1)} %convolution_bitcast_fusion.1), channel_id=1, replica_groups=mesh['leaf_0'=4,'leaf_1'=4,'leaf_2'=2,'group'=16] {'leaf_0','leaf_1','le..., dimensions={0}, use_global_device_ids=true | all-gather | bytes 540672 | tf_op jit(solution)/shard_map/all_gather | solution.py:98
  262.9 2.1 collective-permute-start.3
  264.9 1.1 collective-permute-done.3
  266.0 1.9 collective-permute-start.4
  268.9 4.0 %collective-permute-done.4 = f32[64,512]{1,0:T(8,128)S(1)} collective-permute-done((f32[64,512]{1,0:T(8,128)S(1)}, f32[64,512]{1,0:T(8,128)S(1)}, u32[]{:S(2)}, u32[]{:S(2)}) %collective-permute-start.4) | collective-permute-done | bytes 131104 | tf_op jit(solution)/shard_map/ppermute | solution.py:12
  272.9 3.8 %collective-permute-start.5 = (f32[128,512]{1,0:T(8,128)S(1)}, f32[128,512]{1,0:T(8,128)S(1)}, u32[]{:S(2)}, u32[]{:S(2)}) collective-permute-start(f32[128,512]{1,0:T(8,128)S(1)} %maximum_select_fusion.2), channel_id=1, source_target_pairs={{0,64},{16,80},{32,96},{48,112},{64,0},{80,16},{96,32},{112,48},{1... | collective-permute-start | bytes 786440 | tf_op jit(solution)/shard_map/ppermute | solution.py:12
  276.8 64.2 %all-gather.3.cloned.1.call-done = f32[1,4096,512]{2,1,0:T(8,128)} async-done(((f32[1,128,512]{2,1,0:T(8,128)}), f32[1,4096,512]{2,1,0:T(8,128)}) %all-gather.3.cloned.1.call-update) | async-done | bytes 8388624 | tf_op jit(solution)/shard_map/all_gather | solution.py:77
  341.0 7.0 %gather_fusion = f32[3,1024,512]{2,1,0:T(8,128)} fusion(f32[4,1024,512]{2,1,0:T(8,128)} %bitcast.60, s32[1024]{0:T(1024)S(1)} %pad_clamp_fusion), kind=kCustom, calls=%fused_computation | custom fusion | bytes 12582924 | tf_op jit(solution)/shard_map/jit(_take)/gather | solution.py:79
  348.0 3.6 broadcast_select_fusion
  351.7 10.0 %fusion = f32[512,128]{1,0:T(8,128)S(1)} fusion(f32[3072,512]{1,0:T(8,128)S(1)} %bitcast.59, f32[1,128,3072]{2,1,0:T(8,128)S(1)} %copy-done), kind=kOutput, calls=%fused_computation.2 | convolution fusion | flops 2415919104 | bytes 8126464 | tf_op jit(solution)/shard_map/dot_general | solution.py:63
  361.7 1.0 fusion.5
  (41 shorter events, 4.5 us)
Async XLA Ops:
  6.5 345.1 %copy-start = (f32[1,128,3072]{2,1,0:T(8,128)S(1)}, f32[1,128,3072]{2,1,0:T(8,128)}, u32[]{:S(2)}) copy-start(f32[1,128,3072]{2,1,0:T(8,128)} %param.10) | copy-start | bytes 4718596
  6.5 96.1 %copy-start.6 = (s32[1,4,3]{1,0,2:T(1,128)S(1)}, s32[1,4,3]{1,0,2:T(1,128)}, u32[]{:S(2)}) copy-start(s32[1,4,3]{1,0,2:T(1,128)} %param.14) | copy-start | bytes 148
  6.5 193.8 %copy-start.4 = (f32[1,8,4096]{2,1,0:T(8,128)S(1)}, f32[1,8,4096]{2,1,0:T(8,128)}, u32[]{:S(2)}) copy-start(f32[1,8,4096]{2,1,0:T(8,128)} %param.13) | copy-start | bytes 393220
  6.5 193.8 %all-gather.5.cloned.1.call-start = ((), (), s32[]{:S(2)}) async-start(), calls=%async_computation.5 | async-start | bytes 4456448 | tf_op jit(solution)/shard_map/all_gather | solution.py:96
  8.4 9.2 %collective-permute-start = (f32[128,512]{1,0:T(8,128)S(1)}, f32[128,512]{1,0:T(8,128)S(1)}, u32[]{:S(2)}, u32[]{:S(2)}) collective-permute-start(f32[128,512]{1,0:T(8,128)S(1)} %slice_select_fusion), channel_id=1, source_target_pairs={{0,64},{16,80},{32,96},{48,112},{64,0},{80,16},{96,32},{112,48},{1... | collective-permute-start | bytes 786440 | tf_op jit(solution)/shard_map/ppermute | solution.py:12
  17.7 244.7 %copy-start.5 = (f32[1,32,256]{2,1,0:T(8,128)S(1)}, f32[1,32,256]{2,1,0:T(8,128)}, u32[]{:S(2)}) copy-start(f32[1,32,256]{2,1,0:T(8,128)} %param.12) | copy-start | bytes 98308
  17.7 7.7 %collective-permute-start.1 = (f32[64,512]{1,0:T(8,128)S(1)}, f32[64,512]{1,0:T(8,128)S(1)}, u32[]{:S(2)}, u32[]{:S(2)}) collective-permute-start(f32[64,512]{1,0:T(8,128)S(1)} %slice_select_fusion.1), channel_id=1, source_target_pairs={{0,32},{16,48},{32,0},{48,16},{64,96},{80,112},{96,64},{112,80},{1... | collective-permute-start | bytes 393224 | tf_op jit(solution)/shard_map/ppermute | solution.py:12
  25.4 242.5 %copy-start.1 = (f32[1,128,512]{2,1,0:T(8,128)S(1)}, f32[1,128,512]{2,1,0:T(8,128)}, u32[]{:S(2)}) copy-start(f32[1,128,512]{2,1,0:T(8,128)} %param.8) | copy-start | bytes 786436
  25.4 9.5 %collective-permute-start.2 = (f32[32,512]{1,0:T(8,128)S(1)}, f32[32,512]{1,0:T(8,128)S(1)}, u32[]{:S(2)}, u32[]{:S(2)}) collective-permute-start(f32[32,512]{1,0:T(8,128)S(1)} %slice_select_fusion.2), channel_id=1, source_target_pairs={{0,16},{16,0},{32,48},{48,32},{64,80},{80,64},{96,112},{112,96},{1... | collective-permute-start | bytes 196616 | tf_op jit(solution)/shard_map/ppermute | solution.py:12
  36.3 231.8 %copy-start.3 = (f32[1,128,512]{2,1,0:T(8,128)S(1)}, f32[1,128,512]{2,1,0:T(8,128)}, u32[]{:S(2)}) copy-start(f32[1,128,512]{2,1,0:T(8,128)} %param.9) | copy-start | bytes 786436
  101.9 239.1 %all-gather.3.cloned.1.call-start = ((), (), s32[]{:S(2)}) async-start(), calls=%async_computation.4 | async-start | bytes 8650752 | tf_op jit(solution)/shard_map/all_gather | solution.py:77
  262.9 3.1 collective-permute-start.3
  266.0 6.9 %collective-permute-start.4 = (f32[64,512]{1,0:T(8,128)S(1)}, f32[64,512]{1,0:T(8,128)S(1)}, u32[]{:S(2)}, u32[]{:S(2)}) collective-permute-start(f32[64,512]{1,0:T(8,128)S(1)} %maximum_select_fusion.3), channel_id=1, source_target_pairs={{0,32},{16,48},{32,0},{48,16},{64,96},{80,112},{96,64},{112,80},{1... | collective-permute-start | bytes 393224 | tf_op jit(solution)/shard_map/ppermute | solution.py:12
  272.9 88.8 %collective-permute-start.5 = (f32[128,512]{1,0:T(8,128)S(1)}, f32[128,512]{1,0:T(8,128)S(1)}, u32[]{:S(2)}, u32[]{:S(2)}) collective-permute-start(f32[128,512]{1,0:T(8,128)S(1)} %maximum_select_fusion.2), channel_id=1, source_target_pairs={{0,64},{16,80},{32,96},{48,112},{64,0},{80,16},{96,32},{112,48},{1... | collective-permute-start | bytes 786440 | tf_op jit(solution)/shard_map/ppermute | solution.py:12
  351.6 10.1 %copy-start.2 = (f32[1,128,256]{2,1,0:T(8,128)S(1)}, f32[1,128,256]{2,1,0:T(8,128)}, u32[]{:S(2)}) copy-start(f32[1,128,256]{2,1,0:T(8,128)} %param.11) | copy-start | bytes 393220
Sparse Core Ops, SparseCore 0:
  102.0 98.3 all-gather.4
  203.5 137.4 all-gather.2
where the time goes:
time: 371 us; the launch traced here: 370 us
  waiting for transfers between devices  174 us (47%)
  blocking collectives  123 us (33%)
  starting transfers between devices  27.3 us (7%)
  matrix products  18.5 us (5%)
  between operations  14.4 us (4%)
  local copies, waits for them, and re-layouts  9.16 us (2%)
  other arithmetic  3.88 us (1%)
    all_gather x1, waiting for transfers between devices, shards(): lax.all_gather(group_round, 'group', axis=0, tiled=True).astype(jnp.float32)  97.5 us
    all_gather x1, waiting for transfers between devices, shards(): group_all = lax.all_gather(coefficients, LEAF, axis=1, tiled=True)[0]  64.2 us
    all_gather x1, blocking collectives, shards(): coarse = lax.all_gather(coarse_part, LEAF, axis=0, tiled=True)  58.1 us
    all_to_all x2, blocking collectives, from_everyone(): return lax.all_to_all(copies, axis, split_axis=0, concat_axis=0, tiled=True)  31 us
    all_to_all x1, blocking collectives, sum_by_axis(): return jnp.sum(lax.all_to_all(own, far, 0, 0, tiled=True), axis=0)  29.3 us
    ppermute x6, starting transfers between devices, swapped(): lax.ppermute(shard, axis, [(i, i ^ 1 << distance) for i in range(lax.axis...  27.2 us
    dot_general x6, matrix products, matmul(): jnp.dot(left, right, precision=lax.Precision.HIGHEST, preferred_element_t...  18.5 us
    ppermute x6, waiting for transfers between devices, swapped(): lax.ppermute(shard, axis, [(i, i ^ 1 << distance) for i in range(lax.axis...  12 us
  transfers between devices with their start and end apart: 8, of which 7 were waited for; matrix products, arithmetic and copies ran while one was open for 7% of the time, Pallas kernels for 0%

commit v1 on v0

v1 whole, which is shorter than its diff:
```python
import functools

import jax
import jax.numpy as jnp
from jax import lax
from jax.experimental import pallas as pl
from jax.experimental.pallas import tpu as pltpu
from jax.sharding import PartitionSpec as P

F32 = jnp.float32
BF16 = jnp.bfloat16
I16 = jnp.int16
HIGHEST = lax.Precision.HIGHEST
MESH = pl.DeviceIdType.MESH

ROWS = 128
CODED = ROWS + 16
NEAR = 3
LINKS = 96


def dot(a, b, precision=None):
    return jnp.dot(a, b, precision=precision, preferred_element_type=F32)


def split(a):
    high = a.astype(BF16)
    return high, (a - high.astype(F32)).astype(BF16)


def encode(w):
    peak = jnp.maximum(jnp.max(jnp.abs(w), axis=0, keepdims=True), 1e-30)
    exponent = jnp.ceil(jnp.log2(peak) + 1e-3)
    codes = jnp.round(w * (jnp.exp2(-exponent) * 32767.0))
    codes = jnp.clip(codes, -32767.0, 32767.0).astype(jnp.int32).astype(I16)
    return codes, jnp.broadcast_to(exponent, (16, w.shape[1])).astype(jnp.int32).astype(I16)


def decode(coded):
    codes = coded[:ROWS].astype(jnp.int32).astype(F32)
    exponent = coded[ROWS:].astype(jnp.int32).astype(F32)[:1]
    return codes * (jnp.exp2(exponent) * (1.0 / 32767.0))


def kernel(
    coef, labels, near_kernel, basis, transfer, coupling, lists, ridge, out,
    kraw, khl, wz, wx, near, efull, bmat, cplb, chl, pown, pgive, pgot, hx, rs,
    s1, r1, s2, r2, stack, cgive, cgot, cb, ksem, ssem, rsem,
):
    me = lax.axis_index("leaf")
    g = lax.axis_index("group")
    zh = me // 8
    pos = lax.rem(me, 8)
    x = pos // 2
    c = lax.rem(pos, 2)
    oc = 1 - c
    up, down = lax.rem(zh + 1, 4), lax.rem(zh + 3, 4)
    right, left = lax.rem(x + 1, 4), lax.rem(x + 3, 4)
    beyond = lax.rem(x + 2, 4)
    partner = me + 1 - 2 * c

    def leaf_at(z_, x_, c_):
        return z_ * 8 + x_ * 2 + c_

    to_right, to_left = leaf_at(zh, right, c), leaf_at(zh, left, c)
    to_up, to_down = leaf_at(up, x, c), leaf_at(down, x, c)
    row_peers = [zh * 8 + lax.rem(pos + d, 8) for d in range(1, 8)]
    group_peers = [lax.rem(g + d, 16) for d in range(1, 16)]

    sent = []

    def send(src, dst, leaf=None, group=None):
        i = len(sent)
        target = {"leaf": leaf} if group is None else {"group": group}
        copy = pltpu.make_async_remote_copy(
            src_ref=src, dst_ref=dst, send_sem=ssem.at[i], recv_sem=rsem.at[i],
            device_id=target, device_id_type=MESH,
        )
        copy.start()
        sent.append(copy)
        return copy

    kcopy = pltpu.make_async_copy(near_kernel.at[0], kraw, ksem)
    kcopy.start()

    barrier = pltpu.get_barrier_semaphore()
    for peer in row_peers + [to_up, to_down]:
        pl.semaphore_signal(barrier, inc=1, device_id={"leaf": peer}, device_id_type=MESH)
    for peer in group_peers:
        pl.semaphore_signal(barrier, inc=1, device_id={"group": peer}, device_id_type=MESH)

    codes, exponents = encode(coef[0])
    wz[zh, :ROWS] = codes
    wz[zh, ROWS:] = exponents
    wx[0, x, c, :ROWS] = codes
    wx[0, x, c, ROWS:] = exponents
    cplb[x, c] = coupling[0]
    own_rows = pl.ds(pl.multiple_of(pos * 32, 32), 32)
    efull[own_rows, :] = transfer[0]
    pl.semaphore_wait(barrier, len(row_peers) + 2 + len(group_peers))

    e_in = [send(transfer.at[0], efull.at[own_rows, :], leaf=p) for p in row_peers]
    wz_up = send(wz.at[zh], wz.at[zh], leaf=to_up)
    wz_down = send(wz.at[zh], wz.at[zh], leaf=to_down)

    kcopy.wait()

    @pl.loop(0, 12)
    def _(b):
        high, low = split(kraw[:, pl.ds(pl.multiple_of(b * 256, 256), 256)])
        khl[b, :ROWS] = high
        khl[b, ROWS:] = low

    for copy in e_in:
        copy.wait_recv()
    bm = dot(basis[0], efull[...], HIGHEST)
    bmat[...] = bm
    part = lax.dot_general(
        bm, coef[0], (((0,), (0,)), ((), ())), precision=HIGHEST, preferred_element_type=F32
    )
    low_half, high_half = part[:ROWS], part[ROWS:]
    keep = jnp.where(c == 0, low_half, high_half)
    give = jnp.where(c == 0, high_half, low_half)
    for k in range(4):
        pown[k] = keep[:, k * 128:(k + 1) * 128]
        pgive[k] = give[:, k * 128:(k + 1) * 128]
    core_sum = send(pgive, pgot, leaf=partner)
    core_sum.wait_recv()
    hx[...] = pown[...] + pgot[...]
    rs_in = []
    for d in range(1, 4):
        xd = lax.rem(x + d, 4)
        rs_in.append(send(hx.at[xd], rs.at[d - 1], leaf=leaf_at(zh, xd, c)))

    def gather_start(piece):
        return [send(piece(x), piece(x), leaf=p) for p in (to_right, to_left, partner)]

    def gather_relay(copies, piece, first, second):
        copies[0].wait_recv()
        copies += [
            send(first(left), first(left), leaf=to_right),
            send(piece(left), piece(left), leaf=partner),
        ]
        copies[1].wait_recv()
        copies += [
            send(second(right), second(right), leaf=to_left),
            send(piece(right), piece(right), leaf=partner),
        ]

    def gather_end(copies, piece):
        copies[3].wait_recv()
        copies[5].wait_recv()
        copies.append(send(piece(beyond), piece(beyond), leaf=partner))

    def gather_wait(copies):
        for i in (2, 4, 6, 7):
            copies[i].wait_recv()

    def w_pieces(n):
        return (
            lambda k: wx.at[n, k, c],
            lambda k: wx.at[n, k, c, pl.ds(0, 64)],
            lambda k: wx.at[n, k, c, pl.ds(64, CODED - 64)],
        )

    cpl_pieces = (
        lambda k: cplb.at[k, c],
        lambda k: cplb.at[k, c, :, pl.ds(0, 2048)],
        lambda k: cplb.at[k, c, :, pl.ds(2048, 2048)],
    )

    cpl_g = gather_start(cpl_pieces[0])
    w0 = w_pieces(0)
    w0_g = gather_start(w0[0])

    for copy in rs_in:
        copy.wait_recv()
    s1[...] = (hx[x] + rs[0]) + (rs[1] + rs[2])
    near_z, other_z = leaf_at(zh + 1 - 2 * lax.rem(zh, 2), x, c), leaf_at(3 - zh, x, c)
    lo, hi = pl.ds(0, 64), pl.ds(64, 64)
    ar = [
        send(s1.at[lo], r1.at[lo], leaf=near_z),
        send(s1.at[hi], r1.at[hi], leaf=other_z),
    ]

    gather_relay(w0_g, *w0)
    gather_relay(cpl_g, *cpl_pieces)

    ar[0].wait_recv()
    ar[1].wait_recv()
    s2[...] = s1[...] + r1[...]
    ar += [
        send(s2.at[lo], r2.at[lo], leaf=other_z),
        send(s2.at[hi], r2.at[hi], leaf=near_z),
    ]

    first_rows, last_rows = pl.ds(0, 64), pl.ds(64, CODED - 64)
    wz_up.wait_recv()
    wz_far_up = send(wz.at[down, first_rows], wz.at[down, first_rows], leaf=to_up)
    wz_down.wait_recv()
    wz_far_down = send(wz.at[up, last_rows], wz.at[up, last_rows], leaf=to_down)

    gather_end(w0_g, w0[0])
    gather_end(cpl_g, cpl_pieces[0])

    ar[2].wait_recv()
    ar[3].wait_recv()
    stack[g] = (s2[...] + r2[...]).astype(BF16)
    st_in = [send(stack.at[g], stack.at[g], group=p) for p in group_peers]

    wz_far_up.wait_recv()
    wz_far_down.wait_recv()
    w_g = [w0_g]
    for n in range(1, NEAR):
        wx[n, x, c] = wz[lists[0, zh, n]]
        w_g.append(gather_start(w_pieces(n)[0]))

    def add_near(n):
        @pl.loop(0, 4)
        def _(k):
            b = n * 4 + k
            w = jnp.concatenate([decode(wx[n, k, 0]), decode(wx[n, k, 1])], axis=0)
            high, low = split(w)
            both = dot(khl[b], high)
            term = both[:ROWS] + both[ROWS:] + dot(khl[b, :ROWS], low)
            near[...] += term

    near[...] = jnp.zeros_like(near)
    gather_wait(w0_g)
    add_near(0)

    gather_wait(cpl_g)
    for h in range(16):
        cols = pl.ds(pl.multiple_of(h * 256 + c * 128, 128), 128)
        high, low = split(cplb[:, :, :, cols].reshape(64, 128))
        chl[:64, h * 128:(h + 1) * 128] = high
        chl[64:, h * 128:(h + 1) * 128] = low

    for n in range(1, NEAR):
        gather_relay(w_g[n], *w_pieces(n))

    for copy in st_in:
        copy.wait_recv()
    both = dot(chl[...], stack[...].reshape(2048, 128))
    block = both[:64] + both[64:]
    cgive[...] = jnp.where(c == 0, block[32:], block[:32])
    core_part = jnp.where(c == 0, block[:32], block[32:])
    core_sum2 = send(cgive, cgot, leaf=partner)
    core_sum2.wait_recv()
    cb[x, zh, c] = core_part + cgot[...]
    cz = [
        send(cb.at[x, zh, c], cb.at[x, zh, c], leaf=to_up),
        send(cb.at[x, zh, c], cb.at[x, zh, c], leaf=to_down),
    ]
    for n in range(1, NEAR):
        gather_end(w_g[n], w_pieces(n)[0])
    cz[0].wait_recv()
    cz.append(send(cb.at[x, down, c, pl.ds(0, 16)], cb.at[x, down, c, pl.ds(0, 16)], leaf=to_up))
    cz[1].wait_recv()
    cz.append(send(cb.at[x, up, c, pl.ds(16, 16)], cb.at[x, up, c, pl.ds(16, 16)], leaf=to_down))
    gather_wait(w_g[1])
    add_near(1)
    cz[2].wait_recv()
    cz[3].wait_recv()
    cb_pieces = (
        lambda k: cb.at[k, :, c],
        lambda k: cb.at[k, pl.ds(0, 2), c],
        lambda k: cb.at[k, pl.ds(2, 2), c],
    )
    cb_g = gather_start(cb_pieces[0])
    gather_wait(w_g[2])
    add_near(2)
    gather_relay(cb_g, *cb_pieces)
    gather_end(cb_g, cb_pieces[0])
    gather_wait(cb_g)

    for k in range(4):
        cols = slice(k * 128, (k + 1) * 128)
        far = dot(bmat[...], cb[k].reshape(256, 128), HIGHEST)
        out[0, :, cols] = labels[0, :, cols] - (near[:, cols] + far + ridge[0] * coef[0, :, cols])

    for copy in sent:
        copy.wait_send()


def shards(*operands):
    vmem = pl.BlockSpec(memory_space=pltpu.VMEM)
    smem = pl.BlockSpec(memory_space=pltpu.SMEM)
    v = pltpu.VMEM
    return pl.pallas_call(
        kernel,
        out_shape=jax.ShapeDtypeStruct((1, ROWS, 512), F32),
        in_specs=[vmem, vmem, pl.BlockSpec(memory_space=pl.ANY), vmem, vmem, vmem, smem, smem],
        out_specs=vmem,
        scratch_shapes=[
            v((ROWS, 3072), F32),
            v((12, 256, 256), BF16),
            v((4, CODED, 512), I16),
            v((NEAR, 4, 2, CODED, 512), I16),
            v((ROWS, 512), F32),
            v((256, 256), F32),
            v((ROWS, 256), F32),
            v((4, 2, 8, 4096), F32),
            v((128, 2048), BF16),
            v((4, 128, 128), F32),
            v((4, 128, 128), F32),
            v((4, 128, 128), F32),
            v((4, 128, 128), F32),
            v((3, 128, 128), F32),
            v((128, 128), F32),
            v((128, 128), F32),
            v((128, 128), F32),
            v((128, 128), F32),
            v((16, 128, 128), BF16),
            v((32, 128), F32),
            v((32, 128), F32),
            v((4, 4, 2, 32, 128), F32),
            pltpu.SemaphoreType.DMA,
            pltpu.SemaphoreType.DMA((LINKS,)),
            pltpu.SemaphoreType.DMA((LINKS,)),
        ],
        compiler_params=pltpu.CompilerParams(
            collective_id=0, has_side_effects=True, vmem_limit_bytes=40 * 1024 * 1024
        ),
    )(*operands)


def solution(mesh):
    split_rows = P("group", "leaf", None)
    placed = (split_rows,) * 6 + (P("group", None, None), P())
    return jax.shard_map(
        shards, mesh=mesh, in_specs=placed, out_specs=split_rows, check_vma=False
    )
```

time: 371 us -> 87.4 us (0.24)
  waiting for transfers between devices: 174 us -> 0 us
  blocking collectives: 123 us -> 0 us
  Pallas kernels: 0 us -> 79.1 us
  starting transfers between devices: 27.3 us -> 0 us
  matrix products: 18.5 us -> 0 us
  between operations: 14.4 us -> 0.67 us
  other arithmetic: 3.88 us -> 0 us
    all_gather x2 -> x0, waiting for transfers between devices: 162 us -> none  [the longest x1 97.5 us: shards(): lax.all_gather(group_round, 'group', axis=0, tiled=True).astype(jnp.float32)]
    pallas_call x0 -> x1, Pallas kernels: none -> 79.1 us  [shards(): pl.pallas_call(kernel, out_shape=jax.ShapeDtypeStruct((1, ROWS, 512), F32...]
    all_to_all x4 -> x0, blocking collectives: 64.6 us -> none  [the longest x2 31 us: from_everyone(): return lax.all_to_all(copies, axis, split_axis=0, concat_axis=0, tiled=True)]
    all_gather x1 -> x0, blocking collectives: 58.1 us -> none  [shards(): coarse = lax.all_gather(coarse_part, LEAF, axis=0, tiled=True)]
    ppermute x6 -> x0, starting transfers between devices: 27.2 us -> none  [swapped(): lax.ppermute(shard, axis, [(i, i ^ 1 << distance) for i in range(lax.axis...]
    dot_general x6 -> x0, matrix products: 18.5 us -> none  [matmul(): jnp.dot(left, right, precision=lax.Precision.HIGHEST, preferred_element_t...]
    ppermute x6 -> x0, waiting for transfers between devices: 12 us -> none  [swapped(): lax.ppermute(shard, axis, [(i, i ^ 1 << distance) for i in range(lax.axis...]
    unnamed x16 -> x14, local copies, waits for them, and re-layouts: 0.28 us -> 7.34 us
  transfers between devices with their start and end apart: 8 -> 0, of which waited for: 7 -> 0; matrix products, arithmetic and copies ran while one was open for 7% -> 0% of each run, Pallas kernels for 0% -> 0%
where the time goes in v1:
time: 87.4 us; the launch traced here: 87.1 us
  Pallas kernels  79.1 us (91%)
  local copies, waits for them, and re-layouts  7.34 us (8%)
    pallas_call x1, Pallas kernels, shards(): pl.pallas_call(kernel, out_shape=jax.ShapeDtypeStruct((1, ROWS, 512), F32...  79.1 us
    unnamed x14, local copies, waits for them, and re-layouts  7.34 us

profile of v1, /device:TPU:1, one launch (start us, length us, event | category | flops | bytes accessed | tf_op | source)
XLA Modules:
  0.0 87.1 jit_solution(10625714520978018486)
XLA Ops:
  0.7 0.8 copy.9.lists
  1.4 0.0 copy-start
  1.4 1.4 %copy-done = f32[1,128,3072]{2,1,0:T(8,128)S(1)} copy-done((f32[1,128,3072]{2,1,0:T(8,128)S(1)}, f32[1,128,3072]{2,1,0:T(8,128)}, u32[]{:S(2)}) %copy-start) | copy-done | bytes 1572888
  2.8 0.0 copy-start.1
  2.8 0.9 %copy-done.1 = f32[1,128,512]{2,1,0:T(8,128)S(1)} copy-done((f32[1,128,512]{2,1,0:T(8,128)S(1)}, f32[1,128,512]{2,1,0:T(8,128)}, u32[]{:S(2)}) %copy-start.1) | copy-done | bytes 262168
  3.8 0.0 copy-start.2
  3.8 0.9 %copy-done.2 = f32[1,128,512]{2,1,0:T(8,128)S(1)} copy-done((f32[1,128,512]{2,1,0:T(8,128)S(1)}, f32[1,128,512]{2,1,0:T(8,128)}, u32[]{:S(2)}) %copy-start.2) | copy-done | bytes 262168
  4.7 0.0 copy-start.3
  4.7 0.9 %copy-done.3 = f32[1,128,256]{2,1,0:T(8,128)S(1)} copy-done((f32[1,128,256]{2,1,0:T(8,128)S(1)}, f32[1,128,256]{2,1,0:T(8,128)}, u32[]{:S(2)}) %copy-start.3) | copy-done | bytes 131096
  5.6 0.0 copy-start.4
  5.6 0.9 %copy-done.4 = f32[1,8,4096]{2,1,0:T(8,128)S(1)} copy-done((f32[1,8,4096]{2,1,0:T(8,128)S(1)}, f32[1,8,4096]{2,1,0:T(8,128)}, u32[]{:S(2)}) %copy-start.4) | copy-done | bytes 131096
  6.5 0.0 copy-start.5
  6.5 0.8 copy-done.5
  7.3 79.1 %shard_map.82 = f32[1,128,512]{2,1,0:T(8,128)S(1)} custom-call(f32[1,128,512]{2,1,0:T(8,128)S(1)} %copy-done.1, f32[1,128,512]{2,1,0:T(8,128)S(1)} %copy-done.2, f32[1,128,3072]{2,1,0:T(8,128)S(1)} %copy-done, f32[1,128,256]{2,1,0:T(8,128)S(1)} %copy-done.3, f32[1,32,256]{2,1,0:T(8,128)S(1)} %copy-done.5, f32[1,8,4096]{2,1,0:T(8,128)S(1)} %copy-done.4, ...), custom_call_target="tpu_custom_call" | custom-call | tf_op jit(solution)/shard_map/pallas_call | solution.py:290
  86.4 0.7 copy.12
Async XLA Ops:
  1.4 1.4 %copy-start = (f32[1,128,3072]{2,1,0:T(8,128)S(1)}, f32[1,128,3072]{2,1,0:T(8,128)}, u32[]{:S(2)}) copy-start(f32[1,128,3072]{2,1,0:T(8,128)} %near_kernel.1) | copy-start | bytes 4718596
  2.8 0.9 %copy-start.1 = (f32[1,128,512]{2,1,0:T(8,128)S(1)}, f32[1,128,512]{2,1,0:T(8,128)}, u32[]{:S(2)}) copy-start(f32[1,128,512]{2,1,0:T(8,128)} %coef.1) | copy-start | bytes 786436
  3.8 0.9 %copy-start.2 = (f32[1,128,512]{2,1,0:T(8,128)S(1)}, f32[1,128,512]{2,1,0:T(8,128)}, u32[]{:S(2)}) copy-start(f32[1,128,512]{2,1,0:T(8,128)} %labels.1) | copy-start | bytes 786436
  4.7 0.9 %copy-start.3 = (f32[1,128,256]{2,1,0:T(8,128)S(1)}, f32[1,128,256]{2,1,0:T(8,128)}, u32[]{:S(2)}) copy-start(f32[1,128,256]{2,1,0:T(8,128)} %basis.1) | copy-start | bytes 393220
  5.6 0.9 %copy-start.4 = (f32[1,8,4096]{2,1,0:T(8,128)S(1)}, f32[1,8,4096]{2,1,0:T(8,128)}, u32[]{:S(2)}) copy-start(f32[1,8,4096]{2,1,0:T(8,128)} %coupling.1) | copy-start | bytes 393220
  6.5 0.8 copy-start.5

commit v2 on v1

v2 whole, which is shorter than its diff:
```python
import jax
import jax.numpy as jnp
from jax import lax
from jax.experimental import pallas as pl
from jax.experimental.pallas import tpu as pltpu
from jax.sharding import PartitionSpec as P

F32 = jnp.float32
BF16 = jnp.bfloat16
I16 = jnp.int16
HIGHEST = lax.Precision.HIGHEST
MESH = pl.DeviceIdType.MESH

ROWS = 128
TOP = 6.0
NEAR = 3
LINKS = 128


def dot(a, b, precision=None, dims=((1,), (0,))):
    return lax.dot_general(a, b, (dims, ((), ())), precision=precision, preferred_element_type=F32)


def split(a):
    high = a.astype(BF16)
    return high, (a - high.astype(F32)).astype(BF16)


def encode(w):
    root = jnp.sqrt(jnp.sqrt(jnp.minimum(jnp.abs(w) * (1.0 / TOP), 1.0)))
    return jnp.round(jnp.where(w < 0, -32767.0, 32767.0) * root).astype(jnp.int32).astype(I16)


def decode(codes):
    root = codes.astype(jnp.int32).astype(F32) * (1.0 / 32767.0)
    square = root * root
    return jnp.where(root < 0, -TOP, TOP) * (square * square)


def kernel(
    coef_in, labels_in, near_kernel, basis_in, transfer, coupling, lists_in, ridge, out,
    coef, labels, basis, lists, kraw, khl, wn, wf, wx, near, efull, bmat, cplb, chl,
    pt, pgot, hx, rs, s1, r1, s2, r2, stack, cb, lsem, ssem, rsem,
):
    me = lax.axis_index("leaf")
    g = lax.axis_index("group")
    zh = me // 8
    pos = lax.rem(me, 8)
    x = pos // 2
    c = lax.rem(pos, 2)
    oc = 1 - c
    y = g // 4
    zl = lax.rem(g, 4)

    def turn(i, d):
        return lax.rem(i + d, 4)

    up, down, across = turn(zh, 1), turn(zh, 3), turn(zh, 2)
    right, left, beyond = turn(x, 1), turn(x, 3), turn(x, 2)

    def leaf_at(z_, x_, c_):
        return z_ * 8 + x_ * 2 + c_

    to_right, to_left = leaf_at(zh, right, c), leaf_at(zh, left, c)
    to_up, to_down = leaf_at(up, x, c), leaf_at(down, x, c)
    partner = leaf_at(zh, x, oc)
    row_peers = [zh * 8 + lax.rem(pos + d, 8) for d in range(1, 8)]
    run_peers = [y * 4 + turn(zl, d) for d in range(1, 4)]
    to_north, to_south = turn(y, 1) * 4 + zl, turn(y, 3) * 4 + zl

    sent = []

    def send(src, dst, leaf=None, group=None):
        i = len(sent)
        target = {"leaf": leaf} if group is None else {"group": group}
        copy = pltpu.make_async_remote_copy(
            src_ref=src, dst_ref=dst, send_sem=ssem.at[i], recv_sem=rsem.at[i],
            device_id=target, device_id_type=MESH,
        )
        copy.start()
        sent.append(copy)
        return copy

    def same(ref, leaf=None, group=None):
        return send(ref, ref, leaf, group)

    own_rows = pl.ds(pl.multiple_of(pos * 32, 32), 32)
    loads = [
        pltpu.make_async_copy(src, dst, lsem.at[i])
        for i, (src, dst) in enumerate([
            (coef_in.at[0], coef), (basis_in.at[0], basis), (transfer.at[0], efull.at[own_rows, :]),
            (coupling.at[0], cplb.at[x, c]), (near_kernel.at[0], kraw), (labels_in.at[0], labels),
            (lists_in, lists),
        ])
    ]
    for load in loads:
        load.start()

    barrier = pltpu.get_barrier_semaphore()
    for peer in row_peers + [to_up, to_down]:
        pl.semaphore_signal(barrier, inc=1, device_id={"leaf": peer}, device_id_type=MESH)
    for peer in run_peers + [to_north, to_south]:
        pl.semaphore_signal(barrier, inc=1, device_id={"group": peer}, device_id_type=MESH)

    loads[0].wait()
    loads[1].wait()
    part = dot(coef[...], basis[...], HIGHEST, ((0,), (0,)))
    for k in range(4):
        for h in range(2):
            pt[k, h] = part[(2 * k + h) * 64:(2 * k + h + 1) * 64]
    wx[0, x, c] = encode(coef[...])
    loads[2].wait()
    pl.semaphore_wait(barrier, len(row_peers) + len(run_peers) + 4)

    core_sum = send(pt.at[:, oc], pgot, leaf=partner)

    def gather_start(piece):
        return [same(piece(x), leaf=p) for p in (to_right, to_left, partner)]

    def gather_relay(copies, piece, first, second):
        copies[0].wait_recv()
        copies += [same(first(left), leaf=to_right), same(piece(left), leaf=partner)]
        copies[1].wait_recv()
        copies += [same(second(right), leaf=to_left), same(piece(right), leaf=partner)]

    def gather_end(copies, piece, *_):
        copies[3].wait_recv()
        copies[5].wait_recv()
        copies.append(same(piece(beyond), leaf=partner))

    def gather_wait(copies):
        for i in (2, 4, 6, 7):
            copies[i].wait_recv()

    def e_rows(k, start, size):
        return efull.at[pl.ds(pl.multiple_of((2 * k + c) * 32 + start, 16), size), :]

    e_pieces = (
        lambda k: e_rows(k, 0, 32), lambda k: e_rows(k, 0, 16), lambda k: e_rows(k, 16, 16)
    )
    cpl_pieces = (
        lambda k: cplb.at[k, c],
        lambda k: cplb.at[k, c, :, pl.ds(0, 2048)],
        lambda k: cplb.at[k, c, :, pl.ds(2048, 2048)],
    )

    def w_pieces(n):
        return (
            lambda k: wx.at[n, k, c],
            lambda k: wx.at[n, k, c, pl.ds(0, 64)],
            lambda k: wx.at[n, k, c, pl.ds(64, 64)],
        )

    e_g = gather_start(e_pieces[0])
    w_up = send(wx.at[0, x, c], wn.at[0], leaf=to_up)
    w_down = send(wx.at[0, x, c], wn.at[1], leaf=to_down)
    core_sum.wait_recv()
    hx[...] = pt[:, c] + pgot[...]
    rs_in = [
        send(hx.at[turn(x, d)], rs.at[d - 1], leaf=leaf_at(zh, turn(x, d), c)) for d in range(1, 4)
    ]
    gather_relay(e_g, *e_pieces)
    loads[3].wait()
    cpl_g = gather_start(cpl_pieces[0])
    w_g = [gather_start(w_pieces(0)[0])]
    gather_end(e_g, *e_pieces)
    gather_wait(e_g)

    for copy in rs_in:
        copy.wait_recv()
    group = dot((hx[x] + rs[0]) + (rs[1] + rs[2]), efull[...], HIGHEST).T
    s1[...] = jnp.concatenate([group[:128], group[128:]], axis=1)
    near_z, other_z = leaf_at(zh + 1 - 2 * lax.rem(zh, 2), x, c), leaf_at(3 - zh, x, c)
    lo, hi = pl.ds(0, 64), pl.ds(64, 64)
    ar = [
        send(s1.at[lo], r1.at[lo], leaf=near_z),
        send(s1.at[hi], r1.at[hi], leaf=other_z),
    ]
    bmat[...] = dot(basis[...], efull[...], HIGHEST)
    for load in loads[4:]:
        load.wait()

    @pl.loop(0, 12)
    def _(b):
        high, low = split(kraw[:, pl.ds(pl.multiple_of(b * 256, 256), 256)])
        khl[b, :ROWS] = high
        khl[b, ROWS:] = low

    gather_relay(cpl_g, *cpl_pieces)
    gather_relay(w_g[0], *w_pieces(0))
    ar[0].wait_recv()
    ar[1].wait_recv()
    s2[...] = s1[...] + r1[...]
    ar += [
        send(s2.at[lo], r2.at[lo], leaf=other_z),
        send(s2.at[hi], r2.at[hi], leaf=near_z),
    ]

    w_up.wait_recv()
    far_up = send(wn.at[0, pl.ds(0, 64)], wf.at[pl.ds(0, 64)], leaf=to_up)
    w_down.wait_recv()
    far_down = send(
        wn.at[1, pl.ds(64, 64)], wf.at[pl.ds(64, 64)], leaf=to_down
    )
    one, two = lists[1, 0, zh], lists[2, 0, zh]
    one_adjacent = lax.rem(one + zh, 2)
    adjacent = one_adjacent * one + (1 - one_adjacent) * two
    last = one + two - adjacent
    last_across = 1 - lax.rem(last + zh, 2)
    entry = [0, 2 - one_adjacent, 1 + one_adjacent]
    is_up = lax.rem(adjacent + 4 - zh, 4) == 1
    wx[1, x, c] = jnp.where(is_up, wn[1], wn[0])
    w_g.append(gather_start(w_pieces(1)[0]))
    gather_end(w_g[0], *w_pieces(0))
    gather_end(cpl_g, *cpl_pieces)

    ar[2].wait_recv()
    ar[3].wait_recv()
    stack[g] = (s2[...] + r2[...]).astype(BF16)
    runs = [same(stack.at[g], group=p) for p in run_peers]
    rings = [[same(stack.at[g], group=to_north), same(stack.at[g], group=to_south)]]
    for d in range(1, 4):
        runs[d - 1].wait_recv()
        ref = stack.at[y * 4 + turn(zl, 4 - d)]
        rings.append([same(ref, group=to_north), same(ref, group=to_south)])
    gather_relay(w_g[1], *w_pieces(1))
    for d in range(4):
        zd = turn(zl, 4 - d)
        rings[d][0].wait_recv()
        rings[d].append(same(stack.at[turn(y, 3) * 4 + zd, lo], group=to_north))
        rings[d][1].wait_recv()
        rings[d].append(same(stack.at[turn(y, 1) * 4 + zd, hi], group=to_south))

    far_up.wait_recv()
    far_down.wait_recv()
    other = jnp.where(is_up, wn[0], wn[1])
    wx[2, x, c] = jnp.where(last_across == 1, wf[...], other)
    w_g.append(gather_start(w_pieces(2)[0]))

    def add_near(n):
        @pl.loop(0, 4)
        def _(k):
            b = entry[n] * 4 + k
            w = jnp.concatenate([decode(wx[n, k, 0]), decode(wx[n, k, 1])], axis=0)
            high, low = split(w)
            block = khl[b]
            both = dot(block, high)
            near[...] -= both[:ROWS] + both[ROWS:] + dot(block[:ROWS], low)

    near[...] = labels[...] - ridge[0] * coef[...]
    gather_wait(cpl_g)
    for h in range(16):
        for half in range(2):
            start = h * 256 + half * 128
            high, low = split(cplb[:, :, :, start:start + 128].reshape(64, 128))
            chl[half * 128:half * 128 + 64, h * 128:(h + 1) * 128] = high
            chl[half * 128 + 64:(half + 1) * 128, h * 128:(h + 1) * 128] = low
    gather_wait(w_g[0])
    add_near(0)
    gather_end(w_g[1], *w_pieces(1))

    for ring in rings:
        ring[2].wait_recv()
        ring[3].wait_recv()
    both = dot(chl[...], stack[...].reshape(2048, 128))
    first, second = both[:64] + both[64:128], both[128:192] + both[192:]
    block = first[:, :64] + second[:, 64:]
    cb[zh, pos] = jnp.concatenate([block[:32], block[32:]], axis=1)

    def to_row(z_):
        return [same(cb.at[z_, pos], leaf=p) for p in row_peers]

    cz = [same(cb.at[zh, pos], leaf=p) for p in (to_up, to_down)]
    cb_in = to_row(zh)
    gather_relay(w_g[2], *w_pieces(2))
    cz[0].wait_recv()
    cz.append(same(cb.at[down, pos, pl.ds(0, 16)], leaf=to_up))
    cb_in += to_row(down)
    cz[1].wait_recv()
    cz.append(same(cb.at[up, pos, pl.ds(16, 16)], leaf=to_down))
    cb_in += to_row(up)
    gather_wait(w_g[1])
    add_near(1)
    cz[2].wait_recv()
    cz[3].wait_recv()
    cb_in += to_row(across)
    gather_end(w_g[2], *w_pieces(2))
    gather_wait(w_g[2])
    add_near(2)
    for copy in cb_in:
        copy.wait_recv()

    for k in range(4):
        rows = []
        for z_ in range(4):
            a, b = cb[z_, 2 * k], cb[z_, 2 * k + 1]
            rows += [
                jnp.concatenate([a[:, :64], b[:, :64]], axis=1),
                jnp.concatenate([a[:, 64:], b[:, 64:]], axis=1),
            ]
        cols = slice(k * 128, (k + 1) * 128)
        far = dot(bmat[...], jnp.concatenate(rows, axis=0), HIGHEST)
        out[0, :, cols] = near[:, cols] - far

    for copy in sent:
        copy.wait_send()


def shards(coef, labels, near_kernel, basis, transfer, coupling, lists, ridge):
    operands = coef, labels, near_kernel, basis, transfer, coupling, lists.transpose(2, 0, 1), ridge
    v = pltpu.VMEM
    hbm = pl.BlockSpec(memory_space=pltpu.HBM)
    return pl.pallas_call(
        kernel,
        out_shape=jax.ShapeDtypeStruct((1, ROWS, 512), F32),
        in_specs=[hbm] * 7 + [pl.BlockSpec(memory_space=pltpu.SMEM)],
        out_specs=pl.BlockSpec(memory_space=v),
        scratch_shapes=[
            v((ROWS, 512), F32),
            v((ROWS, 512), F32),
            v((ROWS, 256), F32),
            pltpu.SMEM((NEAR, 1, 4), jnp.int32),
            v((ROWS, 3072), F32),
            v((12, 256, 256), BF16),
            v((2, ROWS, 512), I16),
            v((ROWS, 512), I16),
            v((NEAR, 4, 2, ROWS, 512), I16),
            v((ROWS, 512), F32),
            v((256, 256), F32),
            v((ROWS, 256), F32),
            v((4, 2, 8, 4096), F32),
            v((256, 2048), BF16),
            v((4, 2, 64, 256), F32),
            v((4, 64, 256), F32),
            v((4, 64, 256), F32),
            v((3, 64, 256), F32),
            v((128, 128), F32),
            v((128, 128), F32),
            v((128, 128), F32),
            v((128, 128), F32),
            v((16, 128, 128), BF16),
            v((4, 8, 32, 128), F32),
            pltpu.SemaphoreType.DMA((7,)),
            pltpu.SemaphoreType.DMA((LINKS,)),
            pltpu.SemaphoreType.DMA((LINKS,)),
        ],
        compiler_params=pltpu.CompilerParams(
            collective_id=0, has_side_effects=True, vmem_limit_bytes=67_043_328
        ),
    )(*operands)


def solution(mesh):
    split_rows = P("group", "leaf", None)
    placed = (split_rows,) * 6 + (P("group", None, None), P())
    return jax.shard_map(
        shards, mesh=mesh, in_specs=placed, out_specs=split_rows, check_vma=False
    )
```

time: 87.4 us -> 74.7 us (0.85)
  Pallas kernels: 79.1 us -> 72.2 us
  local copies, waits for them, and re-layouts: 7.34 us -> 1.67 us
    pallas_call x1, Pallas kernels: 79.1 us -> 72.2 us  [shards(): pl.pallas_call(kernel, out_shape=jax.ShapeDtypeStruct((1, ROWS, 512), F32...]
    unnamed x14 -> x1, local copies, waits for them, and re-layouts: 7.34 us -> 1.67 us
where the time goes in v2:
time: 74.7 us; the launch traced here: 74.6 us
  Pallas kernels  72.2 us (97%)
  local copies, waits for them, and re-layouts  1.67 us (2%)
    pallas_call x1, Pallas kernels, shards(): pl.pallas_call(kernel, out_shape=jax.ShapeDtypeStruct((1, ROWS, 512), F32...  72.2 us
    unnamed x1, local copies, waits for them, and re-layouts  1.67 us

profile of v2, /device:TPU:1, one launch (start us, length us, event | category | flops | bytes accessed | tf_op | source)
XLA Modules:
  0.0 74.6 jit_solution(18013585731415984745)
XLA Ops:
  0.7 72.2 %shard_map.82 = f32[1,128,512]{2,1,0:T(8,128)} custom-call(f32[1,128,512]{2,1,0:T(8,128)} %coef_in.1, f32[1,128,512]{2,1,0:T(8,128)} %labels_in.1, f32[1,128,3072]{2,1,0:T(8,128)} %near_kernel.1, f32[1,128,256]{2,1,0:T(8,128)} %basis_in.1, f32[1,32,256]{2,1,0:T(8,128)} %transfer.1, f32[1,8,4096]{2,1,0:T(8,128)} %coupling.1, s32[3,1,4]{2,1,0:T(1,128)} %bitcast.1, ...), custom_call_target="tpu_custom_call" | custom-call | tf_op jit(solution)/shard_map/pallas_call | solution.py:313
  72.9 1.7 %copy.11 = f32[1,128,512]{2,1,0:T(8,128)} copy(f32[1,128,512]{2,1,0:T(8,128)} %shard_map.82) | data formatting | bytes 524288

commit v3 on v2

--- a/solution.py
+++ b/solution.py
@@ -37,10 +37,23 @@
     return jnp.where(root < 0, -TOP, TOP) * (square * square)
 
 
+def pack(v):
+    peak = jnp.maximum(jnp.max(jnp.abs(v), axis=0, keepdims=True), 1e-30)
+    exponent = jnp.ceil(jnp.log2(peak) + 1e-3)
+    codes = jnp.clip(jnp.round(v * (jnp.exp2(-exponent) * 32767.0)), -32767.0, 32767.0)
+    both = jnp.concatenate([codes, jnp.broadcast_to(exponent, (16, v.shape[1]))], axis=0)
+    return both.astype(jnp.int32).astype(I16)
+
+
+def unpack(coded):
+    v = coded.astype(jnp.int32).astype(F32)
+    return v[:-16] * (jnp.exp2(v[-16:-15]) * (1.0 / 32767.0))
+
+
 def kernel(
     coef_in, labels_in, near_kernel, basis_in, transfer, coupling, lists_in, ridge, out,
     coef, labels, basis, lists, kraw, khl, wn, wf, wx, near, efull, bmat, cplb, chl,
-    pt, pgot, hx, rs, s1, r1, s2, r2, stack, cb, lsem, ssem, rsem,
+    pt, pgot, hx, hc, rs, c1, r1, c2, r2, stack, cb, lsem, ssem, rsem,
 ):
     me = lax.axis_index("leaf")
     g = lax.axis_index("group")
@@ -152,12 +165,17 @@
         )
 
     e_g = gather_start(e_pieces[0])
-    w_up = send(wx.at[0, x, c], wn.at[0], leaf=to_up)
-    w_down = send(wx.at[0, x, c], wn.at[1], leaf=to_down)
+    w_in = [
+        send(wx.at[0, x, c, pl.ds(0, 64)], wn.at[0, pl.ds(0, 64)], leaf=to_up),
+        send(wx.at[0, x, c, pl.ds(0, 64)], wn.at[1, pl.ds(0, 64)], leaf=to_down),
+    ]
     core_sum.wait_recv()
-    hx[...] = pt[:, c] + pgot[...]
+    for k in range(4):
+        both = pt[k, c] + pgot[k]
+        hx[k] = jnp.concatenate([both[:, :128], both[:, 128:]], axis=0)
+        hc[k] = pack(hx[k])
     rs_in = [
-        send(hx.at[turn(x, d)], rs.at[d - 1], leaf=leaf_at(zh, turn(x, d), c)) for d in range(1, 4)
+        send(hc.at[turn(x, d)], rs.at[d - 1], leaf=leaf_at(zh, turn(x, d), c)) for d in range(1, 4)
     ]
     gather_relay(e_g, *e_pieces)
     loads[3].wait()
@@ -168,13 +186,20 @@
 
     for copy in rs_in:
         copy.wait_recv()
-    group = dot((hx[x] + rs[0]) + (rs[1] + rs[2]), efull[...], HIGHEST).T
-    s1[...] = jnp.concatenate([group[:128], group[128:]], axis=1)
+    total = (hx[x] + unpack(rs[0])) + (unpack(rs[1]) + unpack(rs[2]))
+    total = jnp.concatenate([total[:64], total[64:]], axis=1)
+    group = dot(total, efull[...], HIGHEST).T
+    group = jnp.concatenate([group[:128], group[128:]], axis=1)
+    c1[0], c1[1] = pack(group[:64]), pack(group[64:])
     near_z, other_z = leaf_at(zh + 1 - 2 * lax.rem(zh, 2), x, c), leaf_at(3 - zh, x, c)
     lo, hi = pl.ds(0, 64), pl.ds(64, 64)
     ar = [
-        send(s1.at[lo], r1.at[lo], leaf=near_z),
-        send(s1.at[hi], r1.at[hi], leaf=other_z),
+        send(c1.at[0], r1.at[0], leaf=near_z),
+        send(c1.at[1], r1.at[1], leaf=other_z),
+    ]
+    w_in += [
+        send(wx.at[0, x, c, pl.ds(64, 64)], wn.at[0, pl.ds(64, 64)], leaf=to_up),
+        send(wx.at[0, x, c, pl.ds(64, 64)], wn.at[1, pl.ds(64, 64)], leaf=to_down),
     ]
     bmat[...] = dot(basis[...], efull[...], HIGHEST)
     for load in loads[4:]:
@@ -190,18 +215,15 @@
     gather_relay(w_g[0], *w_pieces(0))
     ar[0].wait_recv()
     ar[1].wait_recv()
-    s2[...] = s1[...] + r1[...]
+    for h in range(2):
+        c2[h] = pack(unpack(c1[h]) + unpack(r1[h]))
     ar += [
-        send(s2.at[lo], r2.at[lo], leaf=other_z),
-        send(s2.at[hi], r2.at[hi], leaf=near_z),
-    ]
-
-    w_up.wait_recv()
-    far_up = send(wn.at[0, pl.ds(0, 64)], wf.at[pl.ds(0, 64)], leaf=to_up)
-    w_down.wait_recv()
-    far_down = send(
-        wn.at[1, pl.ds(64, 64)], wf.at[pl.ds(64, 64)], leaf=to_down
-    )
+        send(c2.at[0], r2.at[0], leaf=other_z),
+        send(c2.at[1], r2.at[1], leaf=near_z),
+    ]
+
+    for copy in w_in:
+        copy.wait_recv()
     one, two = lists[1, 0, zh], lists[2, 0, zh]
     one_adjacent = lax.rem(one + zh, 2)
     adjacent = one_adjacent * one + (1 - one_adjacent) * two
@@ -216,13 +238,18 @@
 
     ar[2].wait_recv()
     ar[3].wait_recv()
-    stack[g] = (s2[...] + r2[...]).astype(BF16)
+    for h in range(2):
+        stack[g, 64 * h:64 * (h + 1)] = (unpack(c2[h]) + unpack(r2[h])).astype(BF16)
     runs = [same(stack.at[g], group=p) for p in run_peers]
     rings = [[same(stack.at[g], group=to_north), same(stack.at[g], group=to_south)]]
     for d in range(1, 4):
         runs[d - 1].wait_recv()
         ref = stack.at[y * 4 + turn(zl, 4 - d)]
         rings.append([same(ref, group=to_north), same(ref, group=to_south)])
+    far_up = send(wn.at[0, pl.ds(0, 64)], wf.at[pl.ds(0, 64)], leaf=to_up)
+    far_down = send(
+        wn.at[1, pl.ds(64, 64)], wf.at[pl.ds(64, 64)], leaf=to_down
+    )
     gather_relay(w_g[1], *w_pieces(1))
     for d in range(4):
         zd = turn(zl, 4 - d)
@@ -270,19 +297,16 @@
     def to_row(z_):
         return [same(cb.at[z_, pos], leaf=p) for p in row_peers]
 
-    cz = [same(cb.at[zh, pos], leaf=p) for p in (to_up, to_down)]
+    cz = [same(cb.at[zh, pos], leaf=p) for p in (to_up, to_down, leaf_at(across, x, c))]
     cb_in = to_row(zh)
     gather_relay(w_g[2], *w_pieces(2))
     cz[0].wait_recv()
-    cz.append(same(cb.at[down, pos, pl.ds(0, 16)], leaf=to_up))
     cb_in += to_row(down)
     cz[1].wait_recv()
-    cz.append(same(cb.at[up, pos, pl.ds(16, 16)], leaf=to_down))
     cb_in += to_row(up)
     gather_wait(w_g[1])
     add_near(1)
     cz[2].wait_recv()
-    cz[3].wait_recv()
     cb_in += to_row(across)
     gather_end(w_g[2], *w_pieces(2))
     gather_wait(w_g[2])
@@ -332,12 +356,13 @@
             v((256, 2048), BF16),
             v((4, 2, 64, 256), F32),
             v((4, 64, 256), F32),
-            v((4, 64, 256), F32),
-            v((3, 64, 256), F32),
-            v((128, 128), F32),
-            v((128, 128), F32),
-            v((128, 128), F32),
-            v((128, 128), F32),
+            v((4, 128, 128), F32),
+            v((4, 144, 128), I16),
+            v((3, 144, 128), I16),
+            v((2, 80, 128), I16),
+            v((2, 80, 128), I16),
+            v((2, 80, 128), I16),
+            v((2, 80, 128), I16),
             v((16, 128, 128), BF16),
             v((4, 8, 32, 128), F32),
             pltpu.SemaphoreType.DMA((7,)),

time: 74.7 us -> 66.8 us (0.89)
  the two profiles are of different devices: /device:TPU:1 before, /device:TPU:15 now
where the time goes in v3:
time: 66.8 us; the launch traced here: 66.7 us
  Pallas kernels  64.3 us (96%)
  local copies, waits for them, and re-layouts  1.67 us (2%)
    pallas_call x1, Pallas kernels, shards(): pl.pallas_call(kernel, out_shape=jax.ShapeDtypeStruct((1, ROWS, 512), F32...  64.3 us
    unnamed x1, local copies, waits for them, and re-layouts  1.67 us

profile of v3, /device:TPU:15, one launch (start us, length us, event | category | flops | bytes accessed | tf_op | source)
XLA Modules:
  0.0 66.7 jit_solution(1203890231685157870)
XLA Ops:
  0.7 64.3 %shard_map.82 = f32[1,128,512]{2,1,0:T(8,128)} custom-call(f32[1,128,512]{2,1,0:T(8,128)} %coef_in.1, f32[1,128,512]{2,1,0:T(8,128)} %labels_in.1, f32[1,128,3072]{2,1,0:T(8,128)} %near_kernel.1, f32[1,128,256]{2,1,0:T(8,128)} %basis_in.1, f32[1,32,256]{2,1,0:T(8,128)} %transfer.1, f32[1,8,4096]{2,1,0:T(8,128)} %coupling.1, s32[3,1,4]{2,1,0:T(1,128)} %bitcast.1, ...), custom_call_target="tpu_custom_call" | custom-call | tf_op jit(solution)/shard_map/pallas_call | solution.py:337
  65.0 1.7 %copy.11 = f32[1,128,512]{2,1,0:T(8,128)} copy(f32[1,128,512]{2,1,0:T(8,128)} %shard_map.82) | data formatting | bytes 524288

commit v4 on v3

--- a/solution.py
+++ b/solution.py
@@ -77,7 +77,7 @@
     to_right, to_left = leaf_at(zh, right, c), leaf_at(zh, left, c)
     to_up, to_down = leaf_at(up, x, c), leaf_at(down, x, c)
     partner = leaf_at(zh, x, oc)
-    row_peers = [zh * 8 + lax.rem(pos + d, 8) for d in range(1, 8)]
+    row_peers = [zh * 8 + lax.rem(pos + d, 8) for d in (4, 3, 5, 2, 6, 1, 7)]
     run_peers = [y * 4 + turn(zl, d) for d in range(1, 4)]
     to_north, to_south = turn(y, 1) * 4 + zl, turn(y, 3) * 4 + zl
 
@@ -198,8 +198,8 @@
         send(c1.at[1], r1.at[1], leaf=other_z),
     ]
     w_in += [
-        send(wx.at[0, x, c, pl.ds(64, 64)], wn.at[0, pl.ds(64, 64)], leaf=to_up),
-        send(wx.at[0, x, c, pl.ds(64, 64)], wn.at[1, pl.ds(64, 64)], leaf=to_down),
+        send(wx.at[0, x, c, pl.ds(64, 32)], wn.at[0, pl.ds(64, 32)], leaf=to_up),
+        send(wx.at[0, x, c, pl.ds(64, 32)], wn.at[1, pl.ds(64, 32)], leaf=to_down),
     ]
     bmat[...] = dot(basis[...], efull[...], HIGHEST)
     for load in loads[4:]:
@@ -222,7 +222,18 @@
         send(c2.at[1], r2.at[1], leaf=near_z),
     ]
 
-    for copy in w_in:
+    def far_relay(start):
+        first, second = pl.ds(start, 32), pl.ds(start + 32, 32)
+        return [
+            send(wn.at[0, first], wf.at[first], leaf=to_up),
+            send(wn.at[1, second], wf.at[second], leaf=to_down),
+        ]
+
+    w_in += [
+        send(wx.at[0, x, c, pl.ds(96, 32)], wn.at[0, pl.ds(96, 32)], leaf=to_up),
+        send(wx.at[0, x, c, pl.ds(96, 32)], wn.at[1, pl.ds(96, 32)], leaf=to_down),
+    ]
+    for copy in w_in[:2]:
         copy.wait_recv()
     one, two = lists[1, 0, zh], lists[2, 0, zh]
     one_adjacent = lax.rem(one + zh, 2)
@@ -231,8 +242,6 @@
     last_across = 1 - lax.rem(last + zh, 2)
     entry = [0, 2 - one_adjacent, 1 + one_adjacent]
     is_up = lax.rem(adjacent + 4 - zh, 4) == 1
-    wx[1, x, c] = jnp.where(is_up, wn[1], wn[0])
-    w_g.append(gather_start(w_pieces(1)[0]))
     gather_end(w_g[0], *w_pieces(0))
     gather_end(cpl_g, *cpl_pieces)
 
@@ -242,14 +251,15 @@
         stack[g, 64 * h:64 * (h + 1)] = (unpack(c2[h]) + unpack(r2[h])).astype(BF16)
     runs = [same(stack.at[g], group=p) for p in run_peers]
     rings = [[same(stack.at[g], group=to_north), same(stack.at[g], group=to_south)]]
+    for copy in w_in[2:]:
+        copy.wait_recv()
+    wx[1, x, c] = jnp.where(is_up, wn[1], wn[0])
+    w_g.append(gather_start(w_pieces(1)[0]))
     for d in range(1, 4):
         runs[d - 1].wait_recv()
         ref = stack.at[y * 4 + turn(zl, 4 - d)]
         rings.append([same(ref, group=to_north), same(ref, group=to_south)])
-    far_up = send(wn.at[0, pl.ds(0, 64)], wf.at[pl.ds(0, 64)], leaf=to_up)
-    far_down = send(
-        wn.at[1, pl.ds(64, 64)], wf.at[pl.ds(64, 64)], leaf=to_down
-    )
+    far_in = [far_relay(0), far_relay(64)]
     gather_relay(w_g[1], *w_pieces(1))
     for d in range(4):
         zd = turn(zl, 4 - d)
@@ -258,21 +268,34 @@
         rings[d][1].wait_recv()
         rings[d].append(same(stack.at[turn(y, 1) * 4 + zd, hi], group=to_south))
 
-    far_up.wait_recv()
-    far_down.wait_recv()
-    other = jnp.where(is_up, wn[0], wn[1])
-    wx[2, x, c] = jnp.where(last_across == 1, wf[...], other)
-    w_g.append(gather_start(w_pieces(2)[0]))
+    def half_pieces(start):
+        return (
+            lambda k: wx.at[2, k, c, pl.ds(start, 64)],
+            lambda k: wx.at[2, k, c, pl.ds(start, 32)],
+            lambda k: wx.at[2, k, c, pl.ds(start + 32, 32)],
+        )
+
+    def last_start(start):
+        for copy in far_in[start // 64]:
+            copy.wait_recv()
+        rows = slice(start, start + 64)
+        other = jnp.where(is_up, wn[0, rows], wn[1, rows])
+        wx[2, x, c, rows] = jnp.where(last_across == 1, wf[rows], other)
+        return gather_start(half_pieces(start)[0])
+
+    w_g.append(last_start(0))
+
+    def add_block(n, k):
+        w = jnp.concatenate([decode(wx[n, k, 0]), decode(wx[n, k, 1])], axis=0)
+        high, low = split(w)
+        block = khl[entry[n] * 4 + k]
+        both = dot(block, high)
+        near[...] -= both[:ROWS] + both[ROWS:] + dot(block[:ROWS], low)
 
     def add_near(n):
         @pl.loop(0, 4)
         def _(k):
-            b = entry[n] * 4 + k
-            w = jnp.concatenate([decode(wx[n, k, 0]), decode(wx[n, k, 1])], axis=0)
-            high, low = split(w)
-            block = khl[b]
-            both = dot(block, high)
-            near[...] -= both[:ROWS] + both[ROWS:] + dot(block[:ROWS], low)
+            add_block(n, k)
 
     near[...] = labels[...] - ridge[0] * coef[...]
     gather_wait(cpl_g)
@@ -297,20 +320,25 @@
     def to_row(z_):
         return [same(cb.at[z_, pos], leaf=p) for p in row_peers]
 
-    cz = [same(cb.at[zh, pos], leaf=p) for p in (to_up, to_down, leaf_at(across, x, c))]
+    cz = [same(cb.at[zh, pos], leaf=p) for p in (leaf_at(across, x, c), to_up, to_down)]
     cb_in = to_row(zh)
-    gather_relay(w_g[2], *w_pieces(2))
-    cz[0].wait_recv()
+    w_g.append(last_start(64))
+    gather_relay(w_g[2], *half_pieces(0))
+    cz[1].wait_recv()
     cb_in += to_row(down)
-    cz[1].wait_recv()
+    cz[2].wait_recv()
     cb_in += to_row(up)
+    gather_relay(w_g[3], *half_pieces(64))
+    gather_end(w_g[2], *half_pieces(0))
     gather_wait(w_g[1])
     add_near(1)
-    cz[2].wait_recv()
+    cz[0].wait_recv()
     cb_in += to_row(across)
-    gather_end(w_g[2], *w_pieces(2))
-    gather_wait(w_g[2])
-    add_near(2)
+    gather_end(w_g[3], *half_pieces(64))
+    for i, k in ((2, x), (4, left), (6, right), (7, beyond)):
+        w_g[2][i].wait_recv()
+        w_g[3][i].wait_recv()
+        add_block(2, k)
     for copy in cb_in:
         copy.wait_recv()
 

time: 66.8 us -> 66.2 us (level)
  the two profiles are of different devices: /device:TPU:15 before, /device:TPU:1 now
where the time goes in v4:
time: 66.2 us; the launch traced here: 66 us
  Pallas kernels  63.7 us (96%)
  local copies, waits for them, and re-layouts  1.67 us (3%)
    pallas_call x1, Pallas kernels, shards(): pl.pallas_call(kernel, out_shape=jax.ShapeDtypeStruct((1, ROWS, 512), F32...  63.7 us
    unnamed x1, local copies, waits for them, and re-layouts  1.67 us

profile of v4, /device:TPU:1, one launch (start us, length us, event | category | flops | bytes accessed | tf_op | source)
XLA Modules:
  0.0 66.0 jit_solution(3708366139702546612)
XLA Ops:
  0.7 63.7 %shard_map.82 = f32[1,128,512]{2,1,0:T(8,128)} custom-call(f32[1,128,512]{2,1,0:T(8,128)} %coef_in.1, f32[1,128,512]{2,1,0:T(8,128)} %labels_in.1, f32[1,128,3072]{2,1,0:T(8,128)} %near_kernel.1, f32[1,128,256]{2,1,0:T(8,128)} %basis_in.1, f32[1,32,256]{2,1,0:T(8,128)} %transfer.1, f32[1,8,4096]{2,1,0:T(8,128)} %coupling.1, s32[3,1,4]{2,1,0:T(1,128)} %bitcast.1, ...), custom_call_target="tpu_custom_call" | custom-call | tf_op jit(solution)/shard_map/pallas_call | solution.py:365
  64.3 1.7 %copy.11 = f32[1,128,512]{2,1,0:T(8,128)} copy(f32[1,128,512]{2,1,0:T(8,128)} %shard_map.82) | data formatting | bytes 524288

commit v5 on v4

--- a/solution.py
+++ b/solution.py
@@ -52,7 +52,7 @@
 
 def kernel(
     coef_in, labels_in, near_kernel, basis_in, transfer, coupling, lists_in, ridge, out,
-    coef, labels, basis, lists, kraw, khl, wn, wf, wx, near, efull, bmat, cplb, chl,
+    coef, labels, basis, lists, kraw, khl, wn, wf, wx, near, efull, bz, acc, cplb, chl,
     pt, pgot, hx, hc, rs, c1, r1, c2, r2, stack, cb, lsem, ssem, rsem,
 ):
     me = lax.axis_index("leaf")
@@ -201,7 +201,10 @@
         send(wx.at[0, x, c, pl.ds(64, 32)], wn.at[0, pl.ds(64, 32)], leaf=to_up),
         send(wx.at[0, x, c, pl.ds(64, 32)], wn.at[1, pl.ds(64, 32)], leaf=to_down),
     ]
-    bmat[...] = dot(basis[...], efull[...], HIGHEST)
+    high, low = split(dot(basis[...], efull[...], HIGHEST))
+    for z_ in range(4):
+        bz[z_, :ROWS] = high[:, z_ * 64:(z_ + 1) * 64]
+        bz[z_, ROWS:] = low[:, z_ * 64:(z_ + 1) * 64]
     for load in loads[4:]:
         load.wait()
 
@@ -244,6 +247,13 @@
     is_up = lax.rem(adjacent + 4 - zh, 4) == 1
     gather_end(w_g[0], *w_pieces(0))
     gather_end(cpl_g, *cpl_pieces)
+    gather_wait(cpl_g)
+    for h in range(16):
+        for half in range(2):
+            start = h * 256 + half * 128
+            high, low = split(cplb[:, :, :, start:start + 128].reshape(64, 128))
+            chl[half * 128:half * 128 + 64, h * 128:(h + 1) * 128] = high
+            chl[half * 128 + 64:(half + 1) * 128, h * 128:(h + 1) * 128] = low
 
     ar[2].wait_recv()
     ar[3].wait_recv()
@@ -260,6 +270,12 @@
         ref = stack.at[y * 4 + turn(zl, 4 - d)]
         rings.append([same(ref, group=to_north), same(ref, group=to_south)])
     far_in = [far_relay(0), far_relay(64)]
+
+    def coupled(y_):
+        span = pl.ds(pl.multiple_of(y_ * 512, 512), 512)
+        return dot(chl[:, span], stack[pl.ds(y_ * 4, 4)].reshape(512, 128))
+
+    acc[...] = coupled(y)
     gather_relay(w_g[1], *w_pieces(1))
     for d in range(4):
         zd = turn(zl, 4 - d)
@@ -267,6 +283,7 @@
         rings[d].append(same(stack.at[turn(y, 3) * 4 + zd, lo], group=to_north))
         rings[d][1].wait_recv()
         rings[d].append(same(stack.at[turn(y, 1) * 4 + zd, hi], group=to_south))
+    acc[...] += coupled(turn(y, 1)) + coupled(turn(y, 3))
 
     def half_pieces(start):
         return (
@@ -298,13 +315,6 @@
             add_block(n, k)
 
     near[...] = labels[...] - ridge[0] * coef[...]
-    gather_wait(cpl_g)
-    for h in range(16):
-        for half in range(2):
-            start = h * 256 + half * 128
-            high, low = split(cplb[:, :, :, start:start + 128].reshape(64, 128))
-            chl[half * 128:half * 128 + 64, h * 128:(h + 1) * 128] = high
-            chl[half * 128 + 64:(half + 1) * 128, h * 128:(h + 1) * 128] = low
     gather_wait(w_g[0])
     add_near(0)
     gather_end(w_g[1], *w_pieces(1))
@@ -312,7 +322,7 @@
     for ring in rings:
         ring[2].wait_recv()
         ring[3].wait_recv()
-    both = dot(chl[...], stack[...].reshape(2048, 128))
+    both = acc[...] + coupled(turn(y, 2))
     first, second = both[:64] + both[64:128], both[128:192] + both[192:]
     block = first[:, :64] + second[:, 64:]
     cb[zh, pos] = jnp.concatenate([block[:32], block[32:]], axis=1)
@@ -321,45 +331,51 @@
         return [same(cb.at[z_, pos], leaf=p) for p in row_peers]
 
     cz = [same(cb.at[zh, pos], leaf=p) for p in (leaf_at(across, x, c), to_up, to_down)]
-    cb_in = to_row(zh)
+    cb_own = to_row(zh)
     w_g.append(last_start(64))
     gather_relay(w_g[2], *half_pieces(0))
     cz[1].wait_recv()
-    cb_in += to_row(down)
+    cb_down = to_row(down)
     cz[2].wait_recv()
-    cb_in += to_row(up)
+    cb_up = to_row(up)
     gather_relay(w_g[3], *half_pieces(64))
     gather_end(w_g[2], *half_pieces(0))
     gather_wait(w_g[1])
     add_near(1)
+
+    def far_part(copies, z_):
+        for copy in copies:
+            copy.wait_recv()
+        cols = []
+        for k in range(4):
+            a, b = cb[z_, 2 * k], cb[z_, 2 * k + 1]
+            cols.append(jnp.concatenate([
+                jnp.concatenate([a[:, :64], b[:, :64]], axis=1),
+                jnp.concatenate([a[:, 64:], b[:, 64:]], axis=1),
+            ], axis=0))
+        high, low = split(jnp.concatenate(cols, axis=1))
+        both = dot(bz[z_], high)
+        return both[:ROWS] + both[ROWS:] + dot(bz[z_, :ROWS], low)
+
+    near[...] -= far_part(cb_own, zh)
     cz[0].wait_recv()
-    cb_in += to_row(across)
+    cb_across = to_row(across)
     gather_end(w_g[3], *half_pieces(64))
+    near[...] -= far_part(cb_down, down)
+    near[...] -= far_part(cb_up, up)
     for i, k in ((2, x), (4, left), (6, right), (7, beyond)):
         w_g[2][i].wait_recv()
         w_g[3][i].wait_recv()
         add_block(2, k)
-    for copy in cb_in:
-        copy.wait_recv()
-
-    for k in range(4):
-        rows = []
-        for z_ in range(4):
-            a, b = cb[z_, 2 * k], cb[z_, 2 * k + 1]
-            rows += [
-                jnp.concatenate([a[:, :64], b[:, :64]], axis=1),
-                jnp.concatenate([a[:, 64:], b[:, 64:]], axis=1),
-            ]
-        cols = slice(k * 128, (k + 1) * 128)
-        far = dot(bmat[...], jnp.concatenate(rows, axis=0), HIGHEST)
-        out[0, :, cols] = near[:, cols] - far
+    out[0] = near[...] - far_part(cb_across, across)
 
     for copy in sent:
         copy.wait_send()
 
 
 def shards(coef, labels, near_kernel, basis, transfer, coupling, lists, ridge):
-    operands = coef, labels, near_kernel, basis, transfer, coupling, lists.transpose(2, 0, 1), ridge
+    operands = coef, labels, near_kernel, basis, transfer, coupling, lists.transpose(2, 0, 1)
+    operands = [pltpu.with_memory_space_constraint(a, pltpu.HBM) for a in operands]
     v = pltpu.VMEM
     hbm = pl.BlockSpec(memory_space=pltpu.HBM)
     return pl.pallas_call(
@@ -379,7 +395,8 @@
             v((NEAR, 4, 2, ROWS, 512), I16),
             v((ROWS, 512), F32),
             v((256, 256), F32),
-            v((ROWS, 256), F32),
+            v((4, 256, 64), BF16),
+            v((256, 128), F32),
             v((4, 2, 8, 4096), F32),
             v((256, 2048), BF16),
             v((4, 2, 64, 256), F32),
@@ -398,9 +415,9 @@
             pltpu.SemaphoreType.DMA((LINKS,)),
         ],
         compiler_params=pltpu.CompilerParams(
-            collective_id=0, has_side_effects=True, vmem_limit_bytes=67_043_328
+            collective_id=0, has_side_effects=True, vmem_limit_bytes=40 * 1024 * 1024
         ),
-    )(*operands)
+    )(*operands, ridge)
 
 
 def solution(mesh):

time: 66.2 us -> 62.9 us (0.950)
  Pallas kernels: 63.7 us -> 61.2 us
  local copies, waits for them, and re-layouts: 1.67 us -> 0.71 us
    pallas_call x1, Pallas kernels: 63.7 us -> 61.2 us  [shards(): pl.pallas_call(kernel, out_shape=jax.ShapeDtypeStruct((1, ROWS, 512), F32...]
    unnamed x1, local copies, waits for them, and re-layouts: 1.67 us -> 0.71 us
where the time goes in v5:
time: 62.9 us; the launch traced here: 62.5 us
  Pallas kernels  61.2 us (97%)
  local copies, waits for them, and re-layouts  0.71 us (1%)
  between operations  0.66 us (1%)
    pallas_call x1, Pallas kernels, shards(): pl.pallas_call(kernel, out_shape=jax.ShapeDtypeStruct((1, ROWS, 512), F32...  61.2 us

profile of v5, /device:TPU:1, one launch (start us, length us, event | category | flops | bytes accessed | tf_op | source)
XLA Modules:
  0.0 62.5 jit_solution(7045531538603971075)
XLA Ops:
  0.7 61.2 %shard_map.82 = f32[1,128,512]{2,1,0:T(8,128)S(1)} custom-call(f32[1,128,512]{2,1,0:T(8,128)} %coef_in.1, f32[1,128,512]{2,1,0:T(8,128)} %labels_in.1, f32[1,128,3072]{2,1,0:T(8,128)} %near_kernel.1, f32[1,128,256]{2,1,0:T(8,128)} %basis_in.1, f32[1,32,256]{2,1,0:T(8,128)} %transfer.1, f32[1,8,4096]{2,1,0:T(8,128)} %coupling.1, s32[3,1,4]{2,1,0:T(1,128)} %bitcast.1, ...), custom_call_target="tpu_custom_call" | custom-call | tf_op jit(solution)/shard_map/pallas_call | solution.py:381
  61.8 0.7 %copy.11 = f32[1,128,512]{2,1,0:T(8,128)} copy(f32[1,128,512]{2,1,0:T(8,128)S(1)} %shard_map.82) | data formatting | bytes 524288

commit v6 on v5

--- a/solution.py
+++ b/solution.py
@@ -24,6 +24,12 @@
 def split(a):
     high = a.astype(BF16)
     return high, (a - high.astype(F32)).astype(BF16)
+
+
+def dot3(a, b, dims=((1,), (0,))):
+    (a_high, a_low), (b_high, b_low) = split(a), split(b)
+    small = dot(a_low, b_high, None, dims) + dot(a_high, b_low, None, dims)
+    return dot(a_high, b_high, None, dims) + small
 
 
 def encode(w):
@@ -117,7 +123,7 @@
 
     loads[0].wait()
     loads[1].wait()
-    part = dot(coef[...], basis[...], HIGHEST, ((0,), (0,)))
+    part = dot3(coef[...], basis[...], ((0,), (0,)))
     for k in range(4):
         for h in range(2):
             pt[k, h] = part[(2 * k + h) * 64:(2 * k + h + 1) * 64]
@@ -188,7 +194,7 @@
         copy.wait_recv()
     total = (hx[x] + unpack(rs[0])) + (unpack(rs[1]) + unpack(rs[2]))
     total = jnp.concatenate([total[:64], total[64:]], axis=1)
-    group = dot(total, efull[...], HIGHEST).T
+    group = dot3(total, efull[...]).T
     group = jnp.concatenate([group[:128], group[128:]], axis=1)
     c1[0], c1[1] = pack(group[:64]), pack(group[64:])
     near_z, other_z = leaf_at(zh + 1 - 2 * lax.rem(zh, 2), x, c), leaf_at(3 - zh, x, c)

time: 62.9 us -> 63.6 us (1.011)
  the two profiles are of different devices: /device:TPU:1 before, /device:TPU:25 now
where the time goes in v6:
time: 63.6 us; the launch traced here: 63.5 us
  Pallas kernels  62.1 us (98%)
  local copies, waits for them, and re-layouts  0.71 us (1%)
  between operations  0.66 us (1%)
    pallas_call x1, Pallas kernels, shards(): pl.pallas_call(kernel, out_shape=jax.ShapeDtypeStruct((1, ROWS, 512), F32...  62.1 us

profile of v6, /device:TPU:25, one launch (start us, length us, event | category | flops | bytes accessed | tf_op | source)
XLA Modules:
  0.0 63.5 jit_solution(17129025762296406040)
XLA Ops:
  0.7 62.1 %shard_map.82 = f32[1,128,512]{2,1,0:T(8,128)S(1)} custom-call(f32[1,128,512]{2,1,0:T(8,128)} %coef_in.1, f32[1,128,512]{2,1,0:T(8,128)} %labels_in.1, f32[1,128,3072]{2,1,0:T(8,128)} %near_kernel.1, f32[1,128,256]{2,1,0:T(8,128)} %basis_in.1, f32[1,32,256]{2,1,0:T(8,128)} %transfer.1, f32[1,8,4096]{2,1,0:T(8,128)} %coupling.1, s32[3,1,4]{2,1,0:T(1,128)} %bitcast.1, ...), custom_call_target="tpu_custom_call" | custom-call | tf_op jit(solution)/shard_map/pallas_call | solution.py:387
  62.8 0.7 %copy.11 = f32[1,128,512]{2,1,0:T(8,128)} copy(f32[1,128,512]{2,1,0:T(8,128)S(1)} %shard_map.82) | data formatting | bytes 524288
